TPU v7x, 32 devices: a whole 2x2x4 slice. The times are simulated.
32 devices in a mesh: seq: 16 (over z, x, core), fsdp: 2 (over y).
Axes of the slice: x: 2, y: 2, z: 4, core: 2. Of those that a mesh axis runs over, the one named last changes fastest.
Arguments:
- queries: bfloat16 [8192, 2048], P(('seq', 'fsdp')), may hold values from -150 to 150
- key_rotated_rows: bfloat16 [8192, 1024], P(('seq', 'fsdp')), may hold values from -5 to 5
- values: bfloat16 [8192, 1024], P(('seq', 'fsdp')), may hold values from -6 to 6
- out_weight: bfloat16 [2048, 5376], P('seq', 'fsdp'), may hold values from -0.125 to 0.125
- residual: bfloat16 [8192, 5376], P(('seq', 'fsdp')), may hold values from -6 to 6
- norm_gain: float32 [5376], replicated, may hold values from 0.25 to 1.75
- doc_lengths: int32 [8], replicated, may hold values from 1 to 2048, 8192 in all
Outputs:
- output: bfloat16 [8192, 5376], P(('seq', 'fsdp'))
All inputs are finite; a program needn't handle non-finite values.
Results may differ from a plain program's by a relative error of at most 0.007.
Values may be sent and summed in bfloat16 or wider, within the bound.
No kernel may reach another device: no remote copies, remote signals or barrier semaphores. Data moves between devices by JAX's collectives and lax.ppermute only.
A program may use at most 128 MiB of HBM per device.

v0:
```python
import jax
import jax.numpy as jnp
from jax import lax
from jax.sharding import PartitionSpec as P

QUERY_HEADS = 16
KEY_VALUE_HEADS = 8
HEAD_SIZE = 128
WINDOW_TOKENS = 1024
QSCALE = 168


def from_behind(value, axis, by):
    count = lax.axis_size(axis)
    pairs = [(i, i + by) for i in range(count) if 0 <= i + by < count]
    return lax.ppermute(value, axis, pairs)


def doc_index(positions, starts):
    return jnp.sum((starts[None, :] <= positions[:, None]).astype(jnp.int32), axis=1) - 1


def shards(queries, key_rotated_rows, values, out_weight, residual, norm_gain, doc_lengths):
    token_rows = queries.shape[0]
    behind = WINDOW_TOKENS // token_rows
    queries_per_group = QUERY_HEADS // KEY_VALUE_HEADS
    scaling = QSCALE ** (-0.5)
    token_offset = lax.axis_index(("seq", "fsdp")) * token_rows
    starts = jnp.cumsum(doc_lengths) - doc_lengths
    earlier = []
    carried = (key_rotated_rows, values)
    for distance in range(behind):
        carried = from_behind((carried[0], carried[1]), ("seq", "fsdp"), 1)
        earlier.append(carried)
    ordered = earlier[::-1] + [(key_rotated_rows, values)]
    key_gathered = jnp.concatenate([paired[0] for paired in ordered], axis=0)
    value_gathered = jnp.concatenate([paired[1] for paired in ordered], axis=0)
    total_count = key_gathered.shape[0]
    q_pos = token_offset + jnp.arange(token_rows, dtype=jnp.int32)
    k_pos = token_offset - behind * token_rows + jnp.arange(total_count, dtype=jnp.int32)
    q_doc = doc_index(q_pos, starts)
    k_doc = doc_index(k_pos, starts)
    lag = q_pos[:, None] - k_pos[None, :]
    allowed = (
        (q_doc[:, None] == k_doc[None, :])
        & (lag >= 0)
        & (lag < WINDOW_TOKENS)
        & (k_pos[None, :] >= 0)
    )
    last_pos = k_pos[token_rows - 1 :: token_rows]
    live = (last_pos >= 0) & (doc_index(last_pos, starts) == q_doc[0])
    live = jnp.concatenate([live[:-1], jnp.ones((1,), dtype=bool)])
    query_head_rows = queries.reshape(
        token_rows, KEY_VALUE_HEADS, queries_per_group * HEAD_SIZE
    ).transpose(1, 0, 2)
    key_head_rows = key_gathered.reshape(total_count, KEY_VALUE_HEADS, HEAD_SIZE).transpose(1, 0, 2)
    value_head_rows = value_gathered.reshape(total_count, KEY_VALUE_HEADS, HEAD_SIZE).transpose(
        1, 0, 2
    )

    def attend(operands):
        q_head, k_head, v_head = operands
        q_head = q_head.reshape(token_rows, queries_per_group, HEAD_SIZE)
        scores = jnp.einsum("qgd,kd->gqk", q_head, k_head, preferred_element_type=jnp.float32)
        scores = jnp.where(allowed[None], scores * scaling, -jnp.inf)
        peak = jnp.max(scores, axis=-1, keepdims=True)
        expon = jnp.exp(scores - peak)
        probs = (expon / jnp.sum(expon, axis=-1, keepdims=True)).astype(jnp.bfloat16)
        mixed = jnp.einsum("gqk,kd->qgd", probs, v_head, preferred_element_type=jnp.float32)
        return mixed.reshape(token_rows, queries_per_group * HEAD_SIZE)

    heads_out = lax.map(attend, (query_head_rows, key_head_rows, value_head_rows))
    attended = (
        heads_out.transpose(1, 0, 2)
        .reshape(token_rows, QUERY_HEADS * HEAD_SIZE)
        .astype(jnp.bfloat16)
    )
    widened = lax.all_gather(out_weight, "fsdp", axis=1, tiled=True)
    projected = jnp.dot(
        attended,
        lax.all_gather(widened, "seq", axis=0, tiled=True),
        preferred_element_type=jnp.float32,
    )
    meansq = jnp.mean(projected * projected, axis=-1, keepdims=True)
    output = residual.astype(jnp.float32) + norm_gain * projected * lax.rsqrt(meansq + 1e-06)
    return output.astype(jnp.bfloat16)


def solution(mesh):
    in_specs = (
        P(("seq", "fsdp"), None),
        P(("seq", "fsdp"), None),
        P(("seq", "fsdp"), None),
        P("seq", "fsdp"),
        P(("seq", "fsdp"), None),
        P(),
        P(),
    )
    out_specs = P(("seq", "fsdp"), None)
    return jax.shard_map(shards, mesh=mesh, in_specs=in_specs, out_specs=out_specs, check_vma=False)
```

profile of v0, /device:TPU:8, one launch (start us, length us, event | category | flops | bytes accessed | tf_op | source)
XLA Modules:
  0.0 247.7 jit_solution(636366835698399091)
XLA Ops:
  7.3 27.7 %all-gather.3.cloned.1.call-done = bf16[128,5376]{1,0:T(8,128)(2,1)} async-done(((bf16[128,2688]{1,0:T(8,128)(2,1)}), bf16[128,5376]{1,0:T(8,128)(2,1)}) %all-gather.3.cloned.1.call-update) | async-done | bytes 1376272 | tf_op jit(solution)/shard_map/all_gather | solution.py:78
  35.1 2.5 collective-permute-start
  38.8 2.7 %collective-permute-start.4 = (bf16[256,1024]{0,1:T(8,128)(2,1)S(1)}, bf16[256,1024]{0,1:T(8,128)(2,1)S(1)}, u32[]{:S(2)}, u32[]{:S(2)}) collective-permute-start(bf16[256,1024]{0,1:T(8,128)(2,1)S(1)} %copy.20), channel_id=1, source_target_pairs={{0,1},{1,2},{2,3},{3,4},{4,5},{5,6},{6,7},{7,8},{8,9},{9,10},{10,1... | collective-permute-start | bytes 1572872 | tf_op jit(solution)/shard_map/ppermute | solution.py:16
  41.5 9.1 %collective-permute-done = bf16[256,1024]{1,0:T(8,128)(2,1)S(1)} collective-permute-done((bf16[256,1024]{1,0:T(8,128)(2,1)}, bf16[256,1024]{1,0:T(8,128)(2,1)S(1)}, u32[]{:S(2)}, u32[]{:S(2)}) %collective-permute-start) | collective-permute-done | bytes 524320 | tf_op jit(solution)/shard_map/ppermute | solution.py:16
  50.5 3.9 %collective-permute-start.1 = (bf16[256,1024]{1,0:T(8,128)(2,1)S(1)}, bf16[256,1024]{1,0:T(8,128)(2,1)S(1)}, u32[]{:S(2)}, u32[]{:S(2)}) collective-permute-start(bf16[256,1024]{1,0:T(8,128)(2,1)S(1)} %collective-permute-done), channel_id=1, source_target_pairs={{0,1},{1,2},{2,3},{3,4},{4,5},{5,6},{6,7},{7,8},{8,9},{9,10},{10,1... | collective-permute-start | bytes 1572872 | tf_op jit(solution)/shard_map/ppermute | solution.py:16
  56.0 11.4 %collective-permute-done.4 = bf16[256,1024]{0,1:T(8,128)(2,1)S(1)} collective-permute-done((bf16[256,1024]{0,1:T(8,128)(2,1)S(1)}, bf16[256,1024]{0,1:T(8,128)(2,1)S(1)}, u32[]{:S(2)}, u32[]{:S(2)}) %collective-permute-start.4) | collective-permute-done | bytes 524320 | tf_op jit(solution)/shard_map/ppermute | solution.py:16
  69.3 14.9 %collective-permute-done.1 = bf16[256,1024]{1,0:T(8,128)(2,1)S(1)} collective-permute-done((bf16[256,1024]{1,0:T(8,128)(2,1)S(1)}, bf16[256,1024]{1,0:T(8,128)(2,1)S(1)}, u32[]{:S(2)}, u32[]{:S(2)}) %collective-permute-start.1) | collective-permute-done | bytes 524320 | tf_op jit(solution)/shard_map/ppermute | solution.py:16
  86.3 14.7 %collective-permute-done.5 = bf16[256,1024]{0,1:T(8,128)(2,1)S(1)} collective-permute-done((bf16[256,1024]{0,1:T(8,128)(2,1)S(1)}, bf16[256,1024]{0,1:T(8,128)(2,1)S(1)}, u32[]{:S(2)}, u32[]{:S(2)}) %collective-permute-start.5) | collective-permute-done | bytes 524320 | tf_op jit(solution)/shard_map/ppermute | solution.py:16
  103.0 14.9 %collective-permute-done.2 = bf16[256,1024]{1,0:T(8,128)(2,1)S(1)} collective-permute-done((bf16[256,1024]{1,0:T(8,128)(2,1)S(1)}, bf16[256,1024]{1,0:T(8,128)(2,1)S(1)}, u32[]{:S(2)}, u32[]{:S(2)}) %collective-permute-start.2) | collective-permute-done | bytes 524320 | tf_op jit(solution)/shard_map/ppermute | solution.py:16
  119.9 15.0 %collective-permute-done.6 = bf16[256,1024]{0,1:T(8,128)(2,1)} collective-permute-done((bf16[256,1024]{0,1:T(8,128)(2,1)S(1)}, bf16[256,1024]{0,1:T(8,128)(2,1)}, u32[]{:S(2)}, u32[]{:S(2)}) %collective-permute-start.6) | collective-permute-done | bytes 524320 | tf_op jit(solution)/shard_map/ppermute | solution.py:16
  136.8 14.8 %collective-permute-done.3 = bf16[256,1024]{1,0:T(8,128)(2,1)S(1)} collective-permute-done((bf16[256,1024]{1,0:T(8,128)(2,1)S(1)}, bf16[256,1024]{1,0:T(8,128)(2,1)S(1)}, u32[]{:S(2)}, u32[]{:S(2)}) %collective-permute-start.3) | collective-permute-done | bytes 524320 | tf_op jit(solution)/shard_map/ppermute | solution.py:16
  154.0 2.7 %copy.19 = bf16[1280,1024]{0,1:T(8,128)(2,1)} copy(bf16[1280,1024]{1,0:T(8,128)(2,1)S(1)} %constant_dynamic-update-slice_fusion.1) | data formatting | bytes 5242880 | tf_op jit(solution)/shard_map/concatenate | solution.py:37
  156.7 11.9 %collective-permute-done.7 = bf16[256,1024]{0,1:T(8,128)(2,1)} collective-permute-done((bf16[256,1024]{0,1:T(8,128)(2,1)}, bf16[256,1024]{0,1:T(8,128)(2,1)}, u32[]{:S(2)}, u32[]{:S(2)}) %collective-permute-start.7) | collective-permute-done | bytes 524320 | tf_op jit(solution)/shard_map/ppermute | solution.py:16
  176.2 51.0 %while.11 = (s32[]{:T(128)}, bf16[8,256,256]{1,2,0:T(8,128)(2,1)S(1)}, bf16[8,1280,128]{1,2,0:T(8,128)(2,1)}, bf16[8,1280,128]{1,2,0:T(8,128)(2,1)}, bf16[8,256,...) while((s32[]{:T(128)}, ...), condition=%wide.region_6.7_spmd.clone, body=%wide.region_3.6_spmd.clone.sunk | while | flops 511511552 | bytes 2902901 | solution.py:72
  178.2 2.0 fusion.57
  180.2 2.3 fusion.58
  184.6 2.0 fusion.57
  186.6 2.3 fusion.58
  191.0 2.0 fusion.57
  192.9 2.3 fusion.58
  197.4 2.0 fusion.57
  199.3 2.3 fusion.58
  203.7 2.0 fusion.57
  205.7 2.3 fusion.58
  210.1 2.0 fusion.57
  212.1 2.3 fusion.58
  216.5 2.0 fusion.57
  218.5 2.3 fusion.58
  222.9 2.0 fusion.57
  224.9 2.3 fusion.58
  227.3 11.0 %multiply_reduce_fusion = (f32[256]{0:T(256)S(1)}, f32[256,5376]{1,0:T(8,128)S(1)}) fusion(bf16[256,2048]{0,1:T(8,128)(2,1)S(1)} %bitcast.79, bf16[2048,5376]{1,0:T(8,128)(2,1)} %all-gather.5.cloned.1.call-done), kind=kOutput, calls=%fused_computation.29 | convolution fusion | flops 5639897088 | bytes 28574720 | tf_op jit(solution)/shard_map/dot_general | solution.py:79
  238.3 2.5 %add_convert_fusion = bf16[256,5376]{1,0:T(8,128)(2,1)} fusion(f32[256,5376]{1,0:T(8,128)S(1)} %get-tuple-element.106, bf16[256,5376]{1,0:T(8,128)(2,1)S(1)} %copy-done, f32[256]{0:T(256)S(1)} %add_rsqrt_fusion, f32[5376]{0:T(1024)S(1)} %copy-done.9), kind=kLoop, calls=%fused_computation.28 | loop fusion | flops 6881280 | bytes 11032576 | tf_op jit(solution)/shard_map/convert_element_type | solution.py:86
  (79 shorter events, 39.4 us)
Async XLA Ops:
  6.5 47.9 %copy-start.2 = (bf16[256,2048]{1,0:T(8,128)(2,1)S(1)}, bf16[256,2048]{1,0:T(8,128)(2,1)}, u32[]{:S(2)}) copy-start(bf16[256,2048]{1,0:T(8,128)(2,1)} %param.9) | copy-start | bytes 3145732
  6.5 49.2 %copy-start.10 = (s32[8]{0:T(128)S(1)}, s32[8]{0:T(128)}, u32[]{:S(2)}) copy-start(s32[8]{0:T(128)} %param.15) | copy-start | bytes 100
  6.5 28.5 %all-gather.3.cloned.1.call-start = ((), (), s32[]{:S(2)}) async-start(), calls=%async_computation | async-start | bytes 2064384 | tf_op jit(solution)/shard_map/all_gather | solution.py:78
  7.3 220.0 %all-gather.5.cloned.1.call-start = ((), (), s32[]{:S(2)}) async-start(), calls=%async_computation.1 | async-start | bytes 23396352 | tf_op jit(solution)/shard_map/all_gather | solution.py:81
  35.1 15.4 %collective-permute-start = (bf16[256,1024]{1,0:T(8,128)(2,1)}, bf16[256,1024]{1,0:T(8,128)(2,1)S(1)}, u32[]{:S(2)}, u32[]{:S(2)}) collective-permute-start(bf16[256,1024]{1,0:T(8,128)(2,1)} %param.11), channel_id=1, source_target_pairs={{0,1},{1,2},{2,3},{3,4},{4,5},{5,6},{6,7},{7,8},{8,9},{9,10},{10,1... | collective-permute-start | bytes 1572872 | tf_op jit(solution)/shard_map/ppermute | solution.py:16
  38.8 28.6 %collective-permute-start.4 = (bf16[256,1024]{0,1:T(8,128)(2,1)S(1)}, bf16[256,1024]{0,1:T(8,128)(2,1)S(1)}, u32[]{:S(2)}, u32[]{:S(2)}) collective-permute-start(bf16[256,1024]{0,1:T(8,128)(2,1)S(1)} %copy.20), channel_id=1, source_target_pairs={{0,1},{1,2},{2,3},{3,4},{4,5},{5,6},{6,7},{7,8},{8,9},{9,10},{10,1... | collective-permute-start | bytes 1572872 | tf_op jit(solution)/shard_map/ppermute | solution.py:16
  50.5 86.3 %copy-start.5 = (bf16[256,1024]{1,0:T(8,128)(2,1)}, bf16[256,1024]{1,0:T(8,128)(2,1)S(1)}, u32[]{:S(2)}) copy-start(bf16[256,1024]{1,0:T(8,128)(2,1)S(1)} %collective-permute-done) | copy-start | bytes 1572868
  50.5 33.7 %collective-permute-start.1 = (bf16[256,1024]{1,0:T(8,128)(2,1)S(1)}, bf16[256,1024]{1,0:T(8,128)(2,1)S(1)}, u32[]{:S(2)}, u32[]{:S(2)}) collective-permute-start(bf16[256,1024]{1,0:T(8,128)(2,1)S(1)} %collective-permute-done), channel_id=1, source_target_pairs={{0,1},{1,2},{2,3},{3,4},{4,5},{5,6},{6,7},{7,8},{8,9},{9,10},{10,1... | collective-permute-start | bytes 1572872 | tf_op jit(solution)/shard_map/ppermute | solution.py:16
  67.4 69.4 %copy-start.3 = (bf16[256,1024]{0,1:T(8,128)(2,1)}, bf16[256,1024]{0,1:T(8,128)(2,1)S(1)}, u32[]{:S(2)}) copy-start(bf16[256,1024]{0,1:T(8,128)(2,1)S(1)} %collective-permute-done.4) | copy-start | bytes 1572868
  67.4 33.7 %collective-permute-start.5 = (bf16[256,1024]{0,1:T(8,128)(2,1)S(1)}, bf16[256,1024]{0,1:T(8,128)(2,1)S(1)}, u32[]{:S(2)}, u32[]{:S(2)}) collective-permute-start(bf16[256,1024]{0,1:T(8,128)(2,1)S(1)} %collective-permute-done.4), channel_id=1, source_target_pairs={{0,1},{1,2},{2,3},{3,4},{4,5},{5,6},{6,7},{7,8},{8,9},{9,10},{10,1... | collective-permute-start | bytes 1572872 | tf_op jit(solution)/shard_map/ppermute | solution.py:16
  84.2 52.6 %copy-start.7 = (bf16[256,1024]{1,0:T(8,128)(2,1)}, bf16[256,1024]{1,0:T(8,128)(2,1)S(1)}, u32[]{:S(2)}) copy-start(bf16[256,1024]{1,0:T(8,128)(2,1)S(1)} %collective-permute-done.1) | copy-start | bytes 1572868
  84.2 33.7 %collective-permute-start.2 = (bf16[256,1024]{1,0:T(8,128)(2,1)S(1)}, bf16[256,1024]{1,0:T(8,128)(2,1)S(1)}, u32[]{:S(2)}, u32[]{:S(2)}) collective-permute-start(bf16[256,1024]{1,0:T(8,128)(2,1)S(1)} %collective-permute-done.1), channel_id=1, source_target_pairs={{0,1},{1,2},{2,3},{3,4},{4,5},{5,6},{6,7},{7,8},{8,9},{9,10},{10,1... | collective-permute-start | bytes 1572872 | tf_op jit(solution)/shard_map/ppermute | solution.py:16
  101.1 35.8 %copy-start.8 = (bf16[256,1024]{0,1:T(8,128)(2,1)}, bf16[256,1024]{0,1:T(8,128)(2,1)S(1)}, u32[]{:S(2)}) copy-start(bf16[256,1024]{0,1:T(8,128)(2,1)S(1)} %collective-permute-done.5) | copy-start | bytes 1572868
  101.1 33.8 %collective-permute-start.6 = (bf16[256,1024]{0,1:T(8,128)(2,1)S(1)}, bf16[256,1024]{0,1:T(8,128)(2,1)}, u32[]{:S(2)}, u32[]{:S(2)}) collective-permute-start(bf16[256,1024]{0,1:T(8,128)(2,1)S(1)} %collective-permute-done.5), channel_id=1, source_target_pairs={{0,1},{1,2},{2,3},{3,4},{4,5},{5,6},{6,7},{7,8},{8,9},{9,10},{10,1... | collective-permute-start | bytes 1572872 | tf_op jit(solution)/shard_map/ppermute | solution.py:16
  117.9 33.7 %collective-permute-start.3 = (bf16[256,1024]{1,0:T(8,128)(2,1)S(1)}, bf16[256,1024]{1,0:T(8,128)(2,1)S(1)}, u32[]{:S(2)}, u32[]{:S(2)}) collective-permute-start(bf16[256,1024]{1,0:T(8,128)(2,1)S(1)} %collective-permute-done.2), channel_id=1, source_target_pairs={{0,1},{1,2},{2,3},{3,4},{4,5},{5,6},{6,7},{7,8},{8,9},{9,10},{10,1... | collective-permute-start | bytes 1572872 | tf_op jit(solution)/shard_map/ppermute | solution.py:16
  134.9 33.7 %collective-permute-start.7 = (bf16[256,1024]{0,1:T(8,128)(2,1)}, bf16[256,1024]{0,1:T(8,128)(2,1)}, u32[]{:S(2)}, u32[]{:S(2)}) collective-permute-start(bf16[256,1024]{0,1:T(8,128)(2,1)} %collective-permute-done.6), channel_id=1, source_target_pairs={{0,1},{1,2},{2,3},{3,4},{4,5},{5,6},{6,7},{7,8},{8,9},{9,10},{10,1... | collective-permute-start | bytes 1572872 | tf_op jit(solution)/shard_map/ppermute | solution.py:16
  151.6 1.2 copy-start.6
  156.7 17.7 %copy-start.4 = (bf16[256,1024]{0,1:T(8,128)(2,1)S(1)}, bf16[256,1024]{0,1:T(8,128)(2,1)}, u32[]{:S(2)}) copy-start(bf16[256,1024]{0,1:T(8,128)(2,1)} %copy-done.3) | copy-start | bytes 1572868
  156.7 19.5 %copy-start.1 = (bf16[8,256,256]{1,2,0:T(8,128)(2,1)S(1)}, bf16[8,256,256]{1,2,0:T(8,128)(2,1)}, u32[]{:S(2)}) copy-start(bf16[8,256,256]{1,2,0:T(8,128)(2,1)} %custom-call.2) | copy-start | bytes 3145732
  227.3 11.0 %copy-start = (bf16[256,5376]{1,0:T(8,128)(2,1)S(1)}, bf16[256,5376]{1,0:T(8,128)(2,1)}, u32[]{:S(2)}) copy-start(bf16[256,5376]{1,0:T(8,128)(2,1)} %param.13) | copy-start | bytes 8257540
  227.3 11.0 %copy-start.9 = (f32[5376]{0:T(1024)S(1)}, f32[5376]{0:T(1024)}, u32[]{:S(2)}) copy-start(f32[5376]{0:T(1024)} %param.14) | copy-start | bytes 64516
Sparse Core Ops, SparseCore 0:
  8.9 26.1 all-gather.2
  36.6 113.6 all-gather.4
where the time goes:
time: 249 us; the launch traced here: 248 us
  waiting for transfers between devices  135 us (54%)
  matrix products  45.5 us (18%)
  local copies, waits for them, and re-layouts  22.7 us (9%)
  starting transfers between devices  18.6 us (7%)
  between operations  13.7 us (6%)
  other arithmetic  11.7 us (5%)
    ppermute x8, waiting for transfers between devices, from_behind(): return lax.ppermute(value, axis, pairs)  107 us
    all_gather x1, waiting for transfers between devices, shards(): widened = lax.all_gather(out_weight, 'fsdp', axis=1, tiled=True)  27.7 us
    dot_general x8, matrix products, attend(): jnp.einsum('gqk,kd->qgd', probs, v_head, preferred_element_type=jnp.float32)  18.7 us
    ppermute x8, starting transfers between devices, from_behind(): return lax.ppermute(value, axis, pairs)  18.6 us
    sub x8, matrix products, attend(): expon = jnp.exp(scores - peak)  15.8 us
    dot_general x1, matrix products, shards(): jnp.dot(attended, lax.all_gather(widened, 'seq', axis=0, tiled=True), pre...  11 us
    unnamed x32, local copies, waits for them, and re-layouts  10.5 us
    and x8, other arithmetic, shards(): (q_doc[:, None] == k_doc[None, :]) & (lag >= 0) & (lag < WINDOW_TOKENS)  8.73 us
  transfers between devices with their start and end apart: 10, of which 9 were waited for; matrix products, arithmetic and copies ran while one was open for 27% of the time, Pallas kernels for 0%

commit v1 on v0

--- a/solution.py
+++ b/solution.py
@@ -75,7 +75,8 @@
         .reshape(token_rows, QUERY_HEADS * HEAD_SIZE)
         .astype(jnp.bfloat16)
     )
-    widened = lax.all_gather(out_weight, "fsdp", axis=1, tiled=True)
+    pieces = lax.all_gather(out_weight, "fsdp", axis=0, tiled=False)
+    widened = jnp.concatenate(pieces, axis=1)
     projected = jnp.dot(
         attended,
         lax.all_gather(widened, "seq", axis=0, tiled=True),

time: 249 us -> 257 us (1.032); the launches traced: 248 us -> 252 us
    convert_element_type x1, other arithmetic: 2.54 us -> 5.11 us  [shards(): return output.astype(jnp.bfloat16)]
    reshape x0 -> x1, local copies, waits for them, and re-layouts: none -> 2.57 us  [shards(): widened = jnp.concatenate(pieces, axis=1)]
    unnamed x32 -> x36, local copies, waits for them, and re-layouts: 10.5 us -> 9.49 us
  transfers between devices with their start and end apart: 10 -> 10, of which waited for: 9 -> 9; matrix products, arithmetic and copies ran while one was open for 27% -> 26% of each run, Pallas kernels for 0% -> 0%
where the time goes in v1:
time: 257 us; the launch traced here: 252 us
  waiting for transfers between devices  136 us (53%)
  matrix products  47 us (18%)
  local copies, waits for them, and re-layouts  24.2 us (9%)
  starting transfers between devices  16.6 us (6%)
  other arithmetic  14.2 us (6%)
  between operations  13.7 us (5%)
    ppermute x8, waiting for transfers between devices, from_behind(): return lax.ppermute(value, axis, pairs)  108 us
    all_gather x1, waiting for transfers between devices, shards(): pieces = lax.all_gather(out_weight, 'fsdp', axis=0, tiled=False)  27.7 us
    dot_general x8, matrix products, attend(): jnp.einsum('gqk,kd->qgd', probs, v_head, preferred_element_type=jnp.float32)  18.8 us
    ppermute x8, starting transfers between devices, from_behind(): return lax.ppermute(value, axis, pairs)  16.6 us
    sub x8, matrix products, attend(): expon = jnp.exp(scores - peak)  15.8 us
    dot_general x1, matrix products, shards(): jnp.dot(attended, lax.all_gather(widened, 'seq', axis=0, tiled=True), pre...  12.4 us
    unnamed x36, local copies, waits for them, and re-layouts  9.49 us
    and x8, other arithmetic, shards(): (q_doc[:, None] == k_doc[None, :]) & (lag >= 0) & (lag < WINDOW_TOKENS)  8.73 us
  transfers between devices with their start and end apart: 10, of which 9 were waited for; matrix products, arithmetic and copies ran while one was open for 26% of the time, Pallas kernels for 0%

profile of v1, /device:TPU:8, one launch (start us, length us, event | category | flops | bytes accessed | tf_op | source)
XLA Modules:
  0.0 252.4 jit_solution(8918355442045091826)
XLA Ops:
  7.3 27.7 %all-gather.6.cloned.1.call-done = bf16[256,2688]{1,0:T(8,128)(2,1)} async-done(((bf16[128,2688]{1,0:T(8,128)(2,1)}), bf16[256,2688]{1,0:T(8,128)(2,1)}) %all-gather.6.cloned.1.call-update) | async-done | bytes 1376272 | tf_op jit(solution)/shard_map/all_gather | solution.py:78
  35.0 2.6 %copy.32 = bf16[128,2,2688]{0,2,1:T(8,128)(2,1)} copy(bf16[128,2,2688]{2,0,1:T(8,128)(2,1)} %bitcast.84) | data formatting | bytes 2752512 | tf_op jit(solution)/shard_map/reshape | solution.py:79
  37.6 2.5 collective-permute-start
  40.3 2.7 %collective-permute-start.4 = (bf16[256,1024]{0,1:T(8,128)(2,1)S(1)}, bf16[256,1024]{0,1:T(8,128)(2,1)S(1)}, u32[]{:S(2)}, u32[]{:S(2)}) collective-permute-start(bf16[256,1024]{0,1:T(8,128)(2,1)S(1)} %copy.28), channel_id=1, source_target_pairs={{0,1},{1,2},{2,3},{3,4},{4,5},{5,6},{6,7},{7,8},{8,9},{9,10},{10,1... | collective-permute-start | bytes 1572872 | tf_op jit(solution)/shard_map/ppermute | solution.py:16
  43.0 12.4 %collective-permute-done = bf16[256,1024]{1,0:T(8,128)(2,1)S(1)} collective-permute-done((bf16[256,1024]{1,0:T(8,128)(2,1)S(1)}, bf16[256,1024]{1,0:T(8,128)(2,1)S(1)}, u32[]{:S(2)}, u32[]{:S(2)}) %collective-permute-start) | collective-permute-done | bytes 524320 | tf_op jit(solution)/shard_map/ppermute | solution.py:16
  58.8 11.5 %collective-permute-done.4 = bf16[256,1024]{0,1:T(8,128)(2,1)S(1)} collective-permute-done((bf16[256,1024]{0,1:T(8,128)(2,1)S(1)}, bf16[256,1024]{0,1:T(8,128)(2,1)S(1)}, u32[]{:S(2)}, u32[]{:S(2)}) %collective-permute-start.4) | collective-permute-done | bytes 524320 | tf_op jit(solution)/shard_map/ppermute | solution.py:16
  72.2 13.1 %collective-permute-done.1 = bf16[256,1024]{1,0:T(8,128)(2,1)S(1)} collective-permute-done((bf16[256,1024]{1,0:T(8,128)(2,1)S(1)}, bf16[256,1024]{1,0:T(8,128)(2,1)S(1)}, u32[]{:S(2)}, u32[]{:S(2)}) %collective-permute-start.1) | collective-permute-done | bytes 524320 | tf_op jit(solution)/shard_map/ppermute | solution.py:16
  87.5 14.4 %collective-permute-done.5 = bf16[256,1024]{0,1:T(8,128)(2,1)S(1)} collective-permute-done((bf16[256,1024]{0,1:T(8,128)(2,1)S(1)}, bf16[256,1024]{0,1:T(8,128)(2,1)S(1)}, u32[]{:S(2)}, u32[]{:S(2)}) %collective-permute-start.5) | collective-permute-done | bytes 524320 | tf_op jit(solution)/shard_map/ppermute | solution.py:16
  103.8 14.9 %collective-permute-done.2 = bf16[256,1024]{1,0:T(8,128)(2,1)S(1)} collective-permute-done((bf16[256,1024]{1,0:T(8,128)(2,1)S(1)}, bf16[256,1024]{1,0:T(8,128)(2,1)S(1)}, u32[]{:S(2)}, u32[]{:S(2)}) %collective-permute-start.2) | collective-permute-done | bytes 524320 | tf_op jit(solution)/shard_map/ppermute | solution.py:16
  120.6 15.0 %collective-permute-done.6 = bf16[256,1024]{0,1:T(8,128)(2,1)} collective-permute-done((bf16[256,1024]{0,1:T(8,128)(2,1)S(1)}, bf16[256,1024]{0,1:T(8,128)(2,1)}, u32[]{:S(2)}, u32[]{:S(2)}) %collective-permute-start.6) | collective-permute-done | bytes 524320 | tf_op jit(solution)/shard_map/ppermute | solution.py:16
  137.5 14.8 %collective-permute-done.3 = bf16[256,1024]{1,0:T(8,128)(2,1)S(1)} collective-permute-done((bf16[256,1024]{1,0:T(8,128)(2,1)S(1)}, bf16[256,1024]{1,0:T(8,128)(2,1)S(1)}, u32[]{:S(2)}, u32[]{:S(2)}) %collective-permute-start.3) | collective-permute-done | bytes 524320 | tf_op jit(solution)/shard_map/ppermute | solution.py:16
  154.7 2.7 %copy.27 = bf16[1280,1024]{0,1:T(8,128)(2,1)} copy(bf16[1280,1024]{1,0:T(8,128)(2,1)S(1)} %constant_dynamic-update-slice_fusion.1) | data formatting | bytes 5242880 | tf_op jit(solution)/shard_map/concatenate | solution.py:37
  157.4 11.9 %collective-permute-done.7 = bf16[256,1024]{0,1:T(8,128)(2,1)} collective-permute-done((bf16[256,1024]{0,1:T(8,128)(2,1)}, bf16[256,1024]{0,1:T(8,128)(2,1)}, u32[]{:S(2)}, u32[]{:S(2)}) %collective-permute-start.7) | collective-permute-done | bytes 524320 | tf_op jit(solution)/shard_map/ppermute | solution.py:16
  176.9 51.1 %while.11 = (s32[]{:T(128)}, bf16[8,256,256]{1,2,0:T(8,128)(2,1)S(1)}, bf16[8,1280,128]{1,2,0:T(8,128)(2,1)}, bf16[8,1280,128]{1,2,0:T(8,128)(2,1)}, bf16[8,256,...) while((s32[]{:T(128)}, ...), condition=%wide.region_6.7_spmd.clone, body=%wide.region_3.6_spmd.clone.sunk | while | flops 511511552 | bytes 2902901 | solution.py:72
  178.9 2.0 fusion.57
  180.8 2.3 fusion.58
  185.2 2.0 fusion.57
  187.2 2.3 fusion.58
  191.6 2.0 fusion.57
  193.6 2.3 fusion.58
  198.0 2.0 fusion.57
  200.0 2.3 fusion.58
  204.4 2.0 fusion.57
  206.4 2.3 fusion.58
  210.8 2.0 fusion.57
  212.8 2.3 fusion.58
  217.2 2.0 fusion.57
  219.2 2.3 fusion.58
  223.6 2.0 fusion.57
  225.6 2.3 fusion.58
  228.0 12.4 %multiply_reduce_fusion = (f32[256]{0:T(256)S(1)}, f32[256,5376]{1,0:T(8,128)}) fusion(bf16[256,2048]{0,1:T(8,128)(2,1)S(1)} %bitcast.85, bf16[2048,5376]{0,1:T(8,128)(2,1)} %all-gather.4.cloned.1.call-done), kind=kOutput, calls=%fused_computation.29 | convolution fusion | flops 5639897088 | bytes 28574720 | tf_op jit(solution)/shard_map/dot_general | solution.py:80
  240.5 5.1 %add_convert_fusion = bf16[256,5376]{1,0:T(8,128)(2,1)} fusion(f32[256,5376]{1,0:T(8,128)} %get-tuple-element.116, bf16[256,5376]{1,0:T(8,128)(2,1)S(1)} %copy-done, f32[256]{0:T(256)S(1)} %add_rsqrt_fusion, f32[5376]{0:T(1024)S(1)} %copy-done.10), kind=kLoop, calls=%fused_computation.28 | loop fusion | flops 6881280 | bytes 11032576 | tf_op jit(solution)/shard_map/convert_element_type | solution.py:87
  (84 shorter events, 40.3 us)
Async XLA Ops:
  6.5 31.1 %copy-start.3 = (bf16[256,1024]{1,0:T(8,128)(2,1)S(1)}, bf16[256,1024]{1,0:T(8,128)(2,1)}, u32[]{:S(2)}) copy-start(bf16[256,1024]{1,0:T(8,128)(2,1)} %param.11) | copy-start | bytes 1572868
  6.5 33.6 %copy-start.2 = (bf16[256,1024]{1,0:T(8,128)(2,1)S(1)}, bf16[256,1024]{1,0:T(8,128)(2,1)}, u32[]{:S(2)}) copy-start(bf16[256,1024]{1,0:T(8,128)(2,1)} %param.10) | copy-start | bytes 1572868
  6.5 28.5 %all-gather.6.cloned.1.call-start = ((), (), s32[]{:S(2)}) async-start(), calls=%async_computation.1 | async-start | bytes 2064384 | tf_op jit(solution)/shard_map/all_gather | solution.py:78
  7.3 50.1 %copy-start.1 = (bf16[256,2048]{1,0:T(8,128)(2,1)S(1)}, bf16[256,2048]{1,0:T(8,128)(2,1)}, u32[]{:S(2)}) copy-start(bf16[256,2048]{1,0:T(8,128)(2,1)} %param.9) | copy-start | bytes 3145732
  7.3 220.7 %all-gather.4.cloned.1.call-start = ((), (), s32[]{:S(2)}) async-start(), calls=%async_computation | async-start | bytes 23396352 | tf_op jit(solution)/shard_map/all_gather | solution.py:82
  37.6 21.0 %copy-start.12 = (s32[8]{0:T(128)S(1)}, s32[8]{0:T(128)}, u32[]{:S(2)}) copy-start(s32[8]{0:T(128)} %param.15) | copy-start | bytes 100
  37.6 17.7 %collective-permute-start = (bf16[256,1024]{1,0:T(8,128)(2,1)S(1)}, bf16[256,1024]{1,0:T(8,128)(2,1)S(1)}, u32[]{:S(2)}, u32[]{:S(2)}) collective-permute-start(bf16[256,1024]{1,0:T(8,128)(2,1)S(1)} %copy-done.3), channel_id=1, source_target_pairs={{0,1},{1,2},{2,3},{3,4},{4,5},{5,6},{6,7},{7,8},{8,9},{9,10},{10,1... | collective-permute-start | bytes 1572872 | tf_op jit(solution)/shard_map/ppermute | solution.py:16
  40.3 30.0 %collective-permute-start.4 = (bf16[256,1024]{0,1:T(8,128)(2,1)S(1)}, bf16[256,1024]{0,1:T(8,128)(2,1)S(1)}, u32[]{:S(2)}, u32[]{:S(2)}) collective-permute-start(bf16[256,1024]{0,1:T(8,128)(2,1)S(1)} %copy.28), channel_id=1, source_target_pairs={{0,1},{1,2},{2,3},{3,4},{4,5},{5,6},{6,7},{7,8},{8,9},{9,10},{10,1... | collective-permute-start | bytes 1572872 | tf_op jit(solution)/shard_map/ppermute | solution.py:16
  55.4 82.1 %copy-start.6 = (bf16[256,1024]{1,0:T(8,128)(2,1)}, bf16[256,1024]{1,0:T(8,128)(2,1)S(1)}, u32[]{:S(2)}) copy-start(bf16[256,1024]{1,0:T(8,128)(2,1)S(1)} %collective-permute-done) | copy-start | bytes 1572868
  55.4 30.0 %collective-permute-start.1 = (bf16[256,1024]{1,0:T(8,128)(2,1)S(1)}, bf16[256,1024]{1,0:T(8,128)(2,1)S(1)}, u32[]{:S(2)}, u32[]{:S(2)}) collective-permute-start(bf16[256,1024]{1,0:T(8,128)(2,1)S(1)} %collective-permute-done), channel_id=1, source_target_pairs={{0,1},{1,2},{2,3},{3,4},{4,5},{5,6},{6,7},{7,8},{8,9},{9,10},{10,1... | collective-permute-start | bytes 1572872 | tf_op jit(solution)/shard_map/ppermute | solution.py:16
  70.3 67.2 %copy-start.4 = (bf16[256,1024]{0,1:T(8,128)(2,1)}, bf16[256,1024]{0,1:T(8,128)(2,1)S(1)}, u32[]{:S(2)}) copy-start(bf16[256,1024]{0,1:T(8,128)(2,1)S(1)} %collective-permute-done.4) | copy-start | bytes 1572868
  70.3 31.5 %collective-permute-start.5 = (bf16[256,1024]{0,1:T(8,128)(2,1)S(1)}, bf16[256,1024]{0,1:T(8,128)(2,1)S(1)}, u32[]{:S(2)}, u32[]{:S(2)}) collective-permute-start(bf16[256,1024]{0,1:T(8,128)(2,1)S(1)} %collective-permute-done.4), channel_id=1, source_target_pairs={{0,1},{1,2},{2,3},{3,4},{4,5},{5,6},{6,7},{7,8},{8,9},{9,10},{10,1... | collective-permute-start | bytes 1572872 | tf_op jit(solution)/shard_map/ppermute | solution.py:16
  85.4 52.2 %copy-start.8 = (bf16[256,1024]{1,0:T(8,128)(2,1)}, bf16[256,1024]{1,0:T(8,128)(2,1)S(1)}, u32[]{:S(2)}) copy-start(bf16[256,1024]{1,0:T(8,128)(2,1)S(1)} %collective-permute-done.1) | copy-start | bytes 1572868
  85.4 33.3 %collective-permute-start.2 = (bf16[256,1024]{1,0:T(8,128)(2,1)S(1)}, bf16[256,1024]{1,0:T(8,128)(2,1)S(1)}, u32[]{:S(2)}, u32[]{:S(2)}) collective-permute-start(bf16[256,1024]{1,0:T(8,128)(2,1)S(1)} %collective-permute-done.1), channel_id=1, source_target_pairs={{0,1},{1,2},{2,3},{3,4},{4,5},{5,6},{6,7},{7,8},{8,9},{9,10},{10,1... | collective-permute-start | bytes 1572872 | tf_op jit(solution)/shard_map/ppermute | solution.py:16
  101.9 35.7 %copy-start.9 = (bf16[256,1024]{0,1:T(8,128)(2,1)}, bf16[256,1024]{0,1:T(8,128)(2,1)S(1)}, u32[]{:S(2)}) copy-start(bf16[256,1024]{0,1:T(8,128)(2,1)S(1)} %collective-permute-done.5) | copy-start | bytes 1572868
  101.9 33.7 %collective-permute-start.6 = (bf16[256,1024]{0,1:T(8,128)(2,1)S(1)}, bf16[256,1024]{0,1:T(8,128)(2,1)}, u32[]{:S(2)}, u32[]{:S(2)}) collective-permute-start(bf16[256,1024]{0,1:T(8,128)(2,1)S(1)} %collective-permute-done.5), channel_id=1, source_target_pairs={{0,1},{1,2},{2,3},{3,4},{4,5},{5,6},{6,7},{7,8},{8,9},{9,10},{10,1... | collective-permute-start | bytes 1572872 | tf_op jit(solution)/shard_map/ppermute | solution.py:16
  118.6 33.7 %collective-permute-start.3 = (bf16[256,1024]{1,0:T(8,128)(2,1)S(1)}, bf16[256,1024]{1,0:T(8,128)(2,1)S(1)}, u32[]{:S(2)}, u32[]{:S(2)}) collective-permute-start(bf16[256,1024]{1,0:T(8,128)(2,1)S(1)} %collective-permute-done.2), channel_id=1, source_target_pairs={{0,1},{1,2},{2,3},{3,4},{4,5},{5,6},{6,7},{7,8},{8,9},{9,10},{10,1... | collective-permute-start | bytes 1572872 | tf_op jit(solution)/shard_map/ppermute | solution.py:16
  135.6 33.7 %collective-permute-start.7 = (bf16[256,1024]{0,1:T(8,128)(2,1)}, bf16[256,1024]{0,1:T(8,128)(2,1)}, u32[]{:S(2)}, u32[]{:S(2)}) collective-permute-start(bf16[256,1024]{0,1:T(8,128)(2,1)} %collective-permute-done.6), channel_id=1, source_target_pairs={{0,1},{1,2},{2,3},{3,4},{4,5},{5,6},{6,7},{7,8},{8,9},{9,10},{10,1... | collective-permute-start | bytes 1572872 | tf_op jit(solution)/shard_map/ppermute | solution.py:16
  152.3 1.2 copy-start.7
  157.3 17.7 %copy-start.5 = (bf16[256,1024]{0,1:T(8,128)(2,1)S(1)}, bf16[256,1024]{0,1:T(8,128)(2,1)}, u32[]{:S(2)}) copy-start(bf16[256,1024]{0,1:T(8,128)(2,1)} %copy-done.4) | copy-start | bytes 1572868
  157.4 19.5 %copy-start.11 = (bf16[8,256,256]{1,2,0:T(8,128)(2,1)S(1)}, bf16[8,256,256]{1,2,0:T(8,128)(2,1)}, u32[]{:S(2)}) copy-start(bf16[8,256,256]{1,2,0:T(8,128)(2,1)} %custom-call.2) | copy-start | bytes 3145732
  228.0 12.5 %copy-start = (bf16[256,5376]{1,0:T(8,128)(2,1)S(1)}, bf16[256,5376]{1,0:T(8,128)(2,1)}, u32[]{:S(2)}) copy-start(bf16[256,5376]{1,0:T(8,128)(2,1)} %param.13) | copy-start | bytes 8257540
  228.0 12.5 %copy-start.10 = (f32[5376]{0:T(1024)S(1)}, f32[5376]{0:T(1024)}, u32[]{:S(2)}) copy-start(f32[5376]{0:T(1024)} %param.14) | copy-start | bytes 64516
Sparse Core Ops, SparseCore 0:
  8.9 26.1 all-gather.5
  37.8 119.6 all-gather.3
